TPU v7x, 32 devices: a whole 2x2x4 slice. The times are simulated.
32 devices in a mesh: dp: 32 (over z, y, x, core).
Axes of the slice: x: 2, y: 2, z: 4, core: 2. Of those that a mesh axis runs over, the one named last changes fastest.
Arguments:
- params: float32 [4063232], P('dp'), may hold values from -6 to 6
- first_moment: float32 [4063232], P('dp'), may hold values from -2 to 2
- second_moment: float32 [4063232], P('dp'), may hold values from 0.01 to 1
- grads: bfloat16 [4063232], P('dp'), may hold values from -6 to 6
- old_bounds: int32 [33], replicated, may hold values from 0 to 3932160, as said below
- new_bounds: int32 [33], replicated, may hold values from 0 to 3932160, as said below
- seg_start: int32 [64], replicated, may hold values from 0 to 3932096, as said below
Outputs:
- new_params: float32 [4063232], P('dp')
- new_first: float32 [4063232], P('dp')
- new_second: float32 [4063232], P('dp')
Inputs may be any that keep to these rules, and one draw needn't show every extreme that they name: `old_bounds`: starts at 0 and ends at 3932160; every shard holds between 118784 and 126976 elements, exactly 126976 in some shard. `new_bounds`: starts at 0 and ends at 3932160; every shard holds between 118784 and 126976 elements, exactly 126976 in some shard; each entry differs from the same entry of old_bounds by at most 4096, by exactly 4096 somewhere. `seg_start`: strictly rising, the first is 0, all are multiples of 64.
All inputs are finite; a program needn't handle non-finite values.
Results may differ from a plain program's by a relative error of at most 0.0003.
Values sent between devices are 32-bit elements; how exact they have to be, the bound alone decides.
A program may use at most 64 MiB of HBM per device.

v0:
```python
import functools

import jax
import jax.numpy as jnp
from jax import lax
from jax.experimental import pallas as pl
from jax.experimental.pallas import tpu as pltpu
from jax.sharding import PartitionSpec as P

MARGIN = 4096
LANES = 128
BLOCK = MARGIN // LANES
HALF = 64
HALF_BITS = 6
LANE_BITS = 7
PAD = BLOCK + 8
EDGE = 2 * PAD + BLOCK


BETA_ONE = 0.9
BETA_TWO = 0.999
CORR_ONE = 1.0 - 0.9**10
CORR_TWO = 1.0 - 0.999**10
DECAY = 0.01
LEARN = 0.1
EPSILON = 1e-06

MESH = pl.DeviceIdType.MESH
VMEM_LIMIT = 16 * 1024 * 1024


def lane_ids(rows=BLOCK):
    return lax.broadcasted_iota(jnp.int32, (rows, LANES), 1)


def flat_ids():
    return lax.broadcasted_iota(jnp.int32, (BLOCK, LANES), 0) * LANES + lane_ids()


def moved(first, second, lanes):
    picked = jnp.where(lane_ids() >= lanes, first, second)
    return pltpu.roll(picked, (LANES - lanes) & (LANES - 1), 1)


def fetched(tables, refs, sems):
    copies = [pltpu.make_async_copy(t, r, sems.at[i]) for i, (t, r) in enumerate(zip(tables, refs))]
    for copy in copies:
        copy.start()
    return copies


def step_kernel(
    axis, n, old_hbm, new_hbm, seg_hbm, w_hbm, m_hbm, v_hbm, g_hbm, placed, sums, chosen,
    state, m_buf, v_buf, g_buf, squares, member, begins, ends, part, tail, head, left_rim, right_rim,
    before, after, slots, old_ref, new_ref, seg_ref, sems, table_sems, send, receive, rim_send, rim_receive,
):
    rows = m_buf.shape[0]
    blocks = rows // BLOCK
    segs = seg_ref.shape[0]
    me = lax.axis_index(axis)
    right = lax.rem(me + 1, n)
    left = lax.rem(me + n - 1, n)
    tables = fetched((old_hbm, new_hbm, seg_hbm), (old_ref, new_ref, seg_ref), table_sems)
    step_blocks = -(-blocks // sems.shape[1])
    chunks = [(b, min(b + step_blocks, blocks)) for b in range(0, blocks, step_blocks)]
    copies = []
    for c, (b0, b1) in enumerate(chunks):
        window = pl.ds(b0 * BLOCK, (b1 - b0) * BLOCK)
        inside = state.at[0, pl.ds(PAD + b0 * BLOCK, (b1 - b0) * BLOCK)]
        group = [
            pltpu.make_async_copy(w_hbm.at[window], inside, sems.at[0, c]),
            pltpu.make_async_copy(m_hbm.at[window], m_buf.at[window], sems.at[1, c]),
            pltpu.make_async_copy(v_hbm.at[window], v_buf.at[window], sems.at[2, c]),
            pltpu.make_async_copy(g_hbm.at[window], g_buf.at[window], sems.at[3, c]),
        ]
        for copy in group:
            copy.start()
        copies.append(group)

    barrier = pltpu.get_barrier_semaphore()

    def greet(k, carry):
        pl.semaphore_signal(barrier, inc=1, device_id=(lax.rem(me + k, n),), device_id_type=MESH)
        return carry

    lax.fori_loop(1, n, greet, 0)

    for copy in tables:
        copy.wait()
    low = old_ref[me]
    count = old_ref[me + 1] - low
    new_low = new_ref[me]
    new_count = new_ref[me + 1] - new_low
    shift = new_low - low
    phase = (-low) & (HALF - 1)

    def bound_all(origin, offset):
        def bound(s, carry):
            value = (seg_ref[s] - origin - offset) >> HALF_BITS
            begins[pl.ds(s, 1), :] = jnp.full((1, LANES), value, jnp.int32)
            following = (seg_ref[jnp.minimum(s + 1, segs - 1)] - origin - offset) >> HALF_BITS
            following = jnp.where(s + 1 < segs, following, 4 * rows)
            ends[pl.ds(s, 1), :] = jnp.full((1, LANES), following, jnp.int32)
            return carry

        lax.fori_loop(0, segs, bound, 0, unroll=8)

    bound_all(low, phase)
    padded = member.shape[1]
    spot = lane_ids(segs)
    first_half = begins[...]
    past_half = ends[...]
    for group in range(3):
        for tile in range(padded // LANES):
            half = 2 * (spot + tile * LANES) - 1 + group
            mask = (half >= first_half) & (half < past_half)
            member[group * segs : (group + 1) * segs, tile * LANES : (tile + 1) * LANES] = jnp.where(
                mask, 1.0, 0.0
            ).astype(jnp.bfloat16)
    squares[rows:padded, :] = jnp.zeros((padded - rows, 4 * LANES), jnp.bfloat16)

    flat = flat_ids()

    def advance(b, carry):
        here = pl.multiple_of(b * BLOCK, BLOCK)
        there = pl.multiple_of(b * BLOCK + PAD, 8)
        gradient = g_buf[pl.ds(here, BLOCK), :].astype(jnp.float32)
        weight = state[0, pl.ds(there, BLOCK), :]
        moment = BETA_ONE * m_buf[pl.ds(here, BLOCK), :] + (1.0 - BETA_ONE) * gradient
        second = BETA_TWO * v_buf[pl.ds(here, BLOCK), :] + (1.0 - BETA_TWO) * gradient * gradient
        scaled = moment * (1.0 / CORR_ONE)
        update = scaled / (jnp.sqrt(second * (1.0 / CORR_TWO)) + EPSILON) + DECAY * weight
        state[1, pl.ds(there, BLOCK), :] = update
        state[2, pl.ds(there, BLOCK), :] = moment
        state[3, pl.ds(there, BLOCK), :] = second
        live = flat + b * MARGIN < count
        for i, value in enumerate((weight, update)):
            square = jnp.where(live, value * value, 0.0)
            coarse = square.astype(jnp.bfloat16)
            fine = (square - coarse.astype(jnp.float32)).astype(jnp.bfloat16)
            squares[pl.ds(here, BLOCK), i * LANES : (i + 1) * LANES] = coarse
            squares[pl.ds(here, BLOCK), (i + 2) * LANES : (i + 3) * LANES] = fine
        return carry

    for (b0, b1), group in zip(chunks, copies):
        for copy in group:
            copy.wait()
        lax.fori_loop(b0, b1, advance, 0, unroll=2)

    start = count - MARGIN
    start_row = start >> LANE_BITS
    start_lane = start & (LANES - 1)
    for a in range(4):
        head[a] = state[a, PAD : PAD + BLOCK, :]
        tail[a] = moved(
            state[a, pl.ds(PAD + start_row, BLOCK), :],
            state[a, pl.ds(PAD + start_row + 1, BLOCK), :],
            start_lane,
        )

    product = jnp.dot(member[...], squares[...], preferred_element_type=jnp.float32)
    product = product[:, : 2 * LANES] + product[:, 2 * LANES :]
    line = lax.broadcasted_iota(jnp.int32, (segs, LANES), 0)
    row = jnp.zeros((segs, LANES), jnp.float32)
    for i in range(2):
        columns = slice(i * LANES, (i + 1) * LANES)
        mixed = jnp.where(
            spot < phase,
            product[0:segs, columns],
            jnp.where(
                spot < phase + HALF, product[segs : 2 * segs, columns], product[2 * segs : 3 * segs, columns]
            ),
        )
        row = jnp.where(spot == line + i * segs, jnp.sum(mixed, axis=1, keepdims=True), row)
    part[...] = jnp.sum(row, axis=0, keepdims=True)
    pl.semaphore_wait(barrier, n - 1)

    def tell(k):
        return pltpu.make_async_remote_copy(
            src_ref=part,
            dst_ref=slots.at[me],
            send_sem=send,
            recv_sem=receive,
            device_id=(lax.rem(me + k, n),),
            device_id_type=MESH,
        )

    onward = pltpu.make_async_remote_copy(
        src_ref=tail,
        dst_ref=left_rim,
        send_sem=rim_send.at[0],
        recv_sem=rim_receive.at[0],
        device_id=(right,),
        device_id_type=MESH,
    )
    back = pltpu.make_async_remote_copy(
        src_ref=head,
        dst_ref=right_rim,
        send_sem=rim_send.at[1],
        recv_sem=rim_receive.at[1],
        device_id=(left,),
        device_id_type=MESH,
    )

    for k in range(1, n):
        tell(k).start()
    pltpu.make_async_copy(part, slots.at[me], receive).start()
    onward.start()
    back.start()

    top = shift >> LANE_BITS
    lanes = shift & (LANES - 1)

    def own(a, b):
        there = b * BLOCK + PAD + top
        return moved(state[a, pl.ds(there, BLOCK), :], state[a, pl.ds(there + 1, BLOCK), :], lanes)

    def inner(b, carry):
        here = pl.multiple_of(b * BLOCK, BLOCK)
        for a in range(4):
            placed[a, pl.ds(here, BLOCK), :] = own(a, b)
        return carry

    lax.fori_loop(1, blocks - 3, inner, 0, unroll=3)
    for a in range(4):
        before[a, BLOCK:EDGE, :] = state[a, PAD : PAD + EDGE - BLOCK, :]
    onward.wait()
    back.wait()
    for a in range(4):
        before[a, 0:BLOCK, :] = left_rim[a]
        after[a, PAD : PAD + BLOCK, :] = right_rim[a]
    for a in range(4):
        placed[a, 0:BLOCK, :] = moved(
            before[a, pl.ds(BLOCK + top, BLOCK), :], before[a, pl.ds(BLOCK + top + 1, BLOCK), :], lanes
        )

    for b in range(blocks - 3, blocks):
        offset = b * MARGIN + shift - count
        near = jnp.clip(offset >> LANE_BITS, -PAD, PAD - 7) + PAD
        side = offset & (LANES - 1)
        index = flat + b * MARGIN
        beyond = index + shift >= count
        live = index < new_count
        for a in range(4):
            rim = moved(after[a, pl.ds(near, BLOCK), :], after[a, pl.ds(near + 1, BLOCK), :], side)
            value = jnp.where(beyond, rim, own(a, b))
            placed[a, b * BLOCK : (b + 1) * BLOCK, :] = jnp.where(live, value, 0.0)

    new_phase = (-new_low) & (HALF - 1)
    bound_all(new_low, new_phase)
    on_lane = (spot & (segs - 1)) == line
    lows = jnp.sum(jnp.where(on_lane, begins[...], 0), axis=0, keepdims=True)
    highs = jnp.sum(jnp.where(on_lane, ends[...], 0), axis=0, keepdims=True)
    block_row = lax.broadcasted_iota(jnp.int32, (BLOCK, LANES), 0)
    lane_group = lane_ids() >> HALF_BITS

    def choose(b, carry):
        here = pl.multiple_of(b * BLOCK, BLOCK)
        for tile in range(2):
            half = 2 * (block_row + b * BLOCK) - 1 + 2 * tile + lane_group
            mask = (half >= lows) & (half < highs)
            chosen[pl.ds(here, BLOCK), tile * LANES : (tile + 1) * LANES] = jnp.where(mask, 1.0, 0.0).astype(
                jnp.bfloat16
            )
        return carry

    lax.fori_loop(0, blocks, choose, 0, unroll=2)
    sums[1:2, :] = jnp.full((1, LANES), new_phase, jnp.int32).astype(jnp.float32)

    pltpu.make_async_copy(slots, slots, receive).wait()
    sums[0:1, :] = jnp.sum(slots[...], axis=0)
    others = slots.at[pl.ds(0, n - 1)]
    pltpu.make_async_copy(others, others, send).wait()


def apply_kernel(segs, placed, sums, chosen, w_out, m_out, v_out, w_buf, sems):
    m_copy = pltpu.make_async_copy(placed.at[2], m_out, sems.at[0])
    v_copy = pltpu.make_async_copy(placed.at[3], v_out, sems.at[1])
    m_copy.start()
    v_copy.start()
    rows = w_buf.shape[0]
    total = sums[0:1, :]
    phase = sums[1:2, :]
    other = pltpu.roll(total, LANES - segs, 1)
    rate = LEARN * (jnp.sqrt(total) / (jnp.sqrt(other) + EPSILON))
    spot = lane_ids(segs)
    line = lax.broadcasted_iota(jnp.int32, (segs, LANES), 0)
    column = jnp.sum(jnp.where(spot == line, rate, 0.0), axis=1, keepdims=True)
    place = spot.astype(jnp.float32)
    early = place < phase
    late = place >= phase + HALF
    nothing = jnp.zeros((segs, LANES), jnp.float32)
    rates = jnp.concatenate(
        [
            jnp.where(early, column, 0.0),
            jnp.where(early | late, 0.0, column),
            jnp.where(late, column, 0.0),
            nothing,
        ],
        axis=0,
    )
    coarse = rates.astype(jnp.bfloat16)
    fine = (rates - coarse.astype(jnp.float32)).astype(jnp.bfloat16)
    table = jnp.concatenate([coarse, fine], axis=1)
    step = 256
    copies = []
    for c, r0 in enumerate(range(0, rows, step)):
        size = min(step, rows - r0)
        product = jnp.dot(chosen[r0 : r0 + size, :], table, preferred_element_type=jnp.float32)
        factor = product[:, :LANES] + product[:, LANES:]
        w_buf[r0 : r0 + size, :] = placed[0, r0 : r0 + size, :] - factor * placed[1, r0 : r0 + size, :]
        window = pl.ds(r0, size)
        copy = pltpu.make_async_copy(w_buf.at[window], w_out.at[window], sems.at[2 + c])
        copy.start()
        copies.append(copy)
    for copy in (m_copy, v_copy, *copies):
        copy.wait()


def spec(space):
    return pl.BlockSpec(memory_space=space)


def shards(axis, n, params, first_moment, second_moment, grads, old_bounds, new_bounds, seg_start):
    cap = params.shape[0]
    rows = cap // LANES
    f32 = jnp.float32
    flat = [x.reshape(rows, LANES) for x in (params, first_moment, second_moment, grads)]
    old_bounds, new_bounds, seg_start, *flat = (
        pltpu.with_memory_space_constraint(x, pltpu.HBM) for x in (old_bounds, new_bounds, seg_start, *flat)
    )
    segs = seg_start.shape[0]
    padded = -(-rows // 256) * 256
    vmem, hbm = spec(pltpu.VMEM), spec(pltpu.HBM)
    bounds = pltpu.SMEM(old_bounds.shape, jnp.int32)
    starts = pltpu.SMEM(seg_start.shape, jnp.int32)
    rim = pltpu.VMEM((4, BLOCK, LANES), f32)
    dma = pltpu.SemaphoreType.DMA
    placed, sums, chosen = pl.pallas_call(
        functools.partial(step_kernel, axis, n),
        name="step",
        out_shape=(
            jax.ShapeDtypeStruct((4, rows, LANES), f32),
            jax.ShapeDtypeStruct((2, LANES), f32),
            jax.ShapeDtypeStruct((rows, 2 * LANES), jnp.bfloat16),
        ),
        in_specs=[hbm] * 7,
        out_specs=(vmem,) * 3,
        scratch_shapes=[
            pltpu.VMEM((4, rows + 2 * PAD, LANES), f32),
            pltpu.VMEM((rows, LANES), f32),
            pltpu.VMEM((rows, LANES), f32),
            pltpu.VMEM((rows, LANES), grads.dtype),
            pltpu.VMEM((padded, 4 * LANES), jnp.bfloat16),
            pltpu.VMEM((3 * segs, padded), jnp.bfloat16),
            pltpu.VMEM((segs, LANES), jnp.int32),
            pltpu.VMEM((segs, LANES), jnp.int32),
            pltpu.VMEM((1, LANES), f32),
            rim,
            rim,
            rim,
            rim,
            pltpu.VMEM((4, EDGE, LANES), f32),
            pltpu.VMEM((4, EDGE, LANES), f32),
            pltpu.VMEM((n, 1, LANES), f32),
            bounds,
            bounds,
            starts,
            dma((4, 2)),
            dma((3,)),
            dma,
            dma,
            dma((2,)),
            dma((2,)),
        ],
        compiler_params=pltpu.CompilerParams(
            collective_id=0, has_side_effects=True, vmem_limit_bytes=VMEM_LIMIT
        ),
    )(old_bounds, new_bounds, seg_start, *flat)
    whole = jax.ShapeDtypeStruct((rows, LANES), f32)
    outs = pl.pallas_call(
        functools.partial(apply_kernel, segs),
        name="apply",
        out_shape=(whole,) * 3,
        in_specs=[vmem] * 3,
        out_specs=(hbm,) * 3,
        scratch_shapes=[pltpu.VMEM((rows, LANES), f32), dma((2 + -(-rows // 256),))],
        compiler_params=pltpu.CompilerParams(vmem_limit_bytes=VMEM_LIMIT),
    )(placed, sums, chosen)
    return tuple(x.reshape(cap) for x in outs)


def solution(mesh):
    (axis,) = mesh.axis_names
    n = mesh.shape[axis]
    placed = (P(axis), P(axis), P(axis), P(axis), P(), P(), P())
    return jax.shard_map(
        functools.partial(shards, axis, n),
        mesh=mesh,
        in_specs=placed,
        out_specs=(P(axis), P(axis), P(axis)),
        check_vma=False,
    )
```

profile of v0, /device:TPU:0, one launch (start us, length us, event | category | flops | bytes accessed | tf_op | source)
XLA Modules:
  0.0 14.0 jit_solution(10435601412703746565)
XLA Ops:
  0.6 12.1 %step.1 = (f32[4,992,128]{2,1,0:T(8,128)S(1)}, f32[2,128]{1,0:T(2,128)S(1)}, bf16[992,256]{1,0:T(8,128)(2,1)S(1)}) custom-call(s32[33]{0:T(128)} %old_hbm.1, s32[33]{0:T(128)} %new_hbm.1, s32[64]{0:T(128)} %seg_hbm.1, f32[992,128]{1,0:T(8,128)} %bitcast.7, f32[992,128]{1,0:T(8,128)} %bitcast.8, f32[992,128]{1,0:T(8,128)} %bitcast.9, bf16[992,128]{1,0:T(8,128)(2,1)} %bitcast.10), custom_call_target="tpu_custom_call" | custom-call | tf_op jit(solution)/shard_map/step/pallas_call | solution.py:339
  12.7 1.2 %apply.1 = (f32[992,128]{1,0:T(8,128)}, f32[992,128]{1,0:T(8,128)}, f32[992,128]{1,0:T(8,128)}) custom-call(f32[4,992,128]{2,1,0:T(8,128)S(1)} %get-tuple-element.9.placed, f32[2,128]{1,0:T(2,128)S(1)} %get-tuple-element.10.sums, bf16[992,256]{1,0:T(8,128)(2,1)S(1)} %get-tuple-element.11.chosen), custom_call_target="tpu_custom_call" | custom-call | tf_op jit(solution)/shard_map/apply/pallas_call | solution.py:381
where the time goes:
time: 14.1 us; the launch traced here: 14 us
  Pallas kernels  13.3 us (94%)
  between operations  0.64 us (5%)
    pallas_call x1, Pallas kernels, shards(): pl.pallas_call(functools.partial(step_kernel, axis, n), name='step', out_...  12.1 us
    pallas_call x1, Pallas kernels, shards(): pl.pallas_call(functools.partial(apply_kernel, segs), name='apply', out_s...  1.24 us

commit v1 on v0

--- a/solution.py
+++ b/solution.py
@@ -205,8 +205,14 @@
     for k in range(1, n):
         tell(k).start()
     pltpu.make_async_copy(part, slots.at[me], receive).start()
-    onward.start()
-    back.start()
+
+    @pl.when(me < n - 1)
+    def send_tail():
+        onward.start()
+
+    @pl.when(me > 0)
+    def send_head():
+        back.start()
 
     top = shift >> LANE_BITS
     lanes = shift & (LANES - 1)
@@ -224,8 +230,17 @@
     lax.fori_loop(1, blocks - 3, inner, 0, unroll=3)
     for a in range(4):
         before[a, BLOCK:EDGE, :] = state[a, PAD : PAD + EDGE - BLOCK, :]
-    onward.wait()
-    back.wait()
+
+    @pl.when(me < n - 1)
+    def end_right():
+        onward.wait_send()
+        back.wait_recv()
+
+    @pl.when(me > 0)
+    def end_left():
+        back.wait_send()
+        onward.wait_recv()
+
     for a in range(4):
         before[a, 0:BLOCK, :] = left_rim[a]
         after[a, PAD : PAD + BLOCK, :] = right_rim[a]

time: 14.1 us -> 13.3 us (0.943)
  Pallas kernels: 13.3 us -> 12.5 us
    pallas_call x1, Pallas kernels: 12.1 us -> 11.2 us  [shards(): pl.pallas_call(functools.partial(step_kernel, axis, n), name='step', out_...]
where the time goes in v1:
time: 13.3 us; the launch traced here: 13.1 us
  Pallas kernels  12.5 us (94%)
  between operations  0.64 us (5%)
    pallas_call x1, Pallas kernels, shards(): pl.pallas_call(functools.partial(step_kernel, axis, n), name='step', out_...  11.2 us
    pallas_call x1, Pallas kernels, shards(): pl.pallas_call(functools.partial(apply_kernel, segs), name='apply', out_s...  1.24 us

profile of v1, /device:TPU:0, one launch (start us, length us, event | category | flops | bytes accessed | tf_op | source)
XLA Modules:
  0.0 13.1 jit_solution(13995726486402532598)
XLA Ops:
  0.6 11.2 %step.1 = (f32[4,992,128]{2,1,0:T(8,128)S(1)}, f32[2,128]{1,0:T(2,128)S(1)}, bf16[992,256]{1,0:T(8,128)(2,1)S(1)}) custom-call(s32[33]{0:T(128)} %old_hbm.1, s32[33]{0:T(128)} %new_hbm.1, s32[64]{0:T(128)} %seg_hbm.1, f32[992,128]{1,0:T(8,128)} %bitcast.7, f32[992,128]{1,0:T(8,128)} %bitcast.8, f32[992,128]{1,0:T(8,128)} %bitcast.9, bf16[992,128]{1,0:T(8,128)(2,1)} %bitcast.10), custom_call_target="tpu_custom_call" | custom-call | tf_op jit(solution)/shard_map/step/pallas_call | solution.py:354
  11.9 1.2 %apply.1 = (f32[992,128]{1,0:T(8,128)}, f32[992,128]{1,0:T(8,128)}, f32[992,128]{1,0:T(8,128)}) custom-call(f32[4,992,128]{2,1,0:T(8,128)S(1)} %get-tuple-element.9.placed, f32[2,128]{1,0:T(2,128)S(1)} %get-tuple-element.10.sums, bf16[992,256]{1,0:T(8,128)(2,1)S(1)} %get-tuple-element.11.chosen), custom_call_target="tpu_custom_call" | custom-call | tf_op jit(solution)/shard_map/apply/pallas_call | solution.py:396

commit v2 on v1

--- a/solution.py
+++ b/solution.py
@@ -15,6 +15,7 @@
 LANE_BITS = 7
 PAD = BLOCK + 8
 EDGE = 2 * PAD + BLOCK
+TILE = 256
 
 
 BETA_ONE = 0.9
@@ -51,31 +52,29 @@
 
 def step_kernel(
     axis, n, old_hbm, new_hbm, seg_hbm, w_hbm, m_hbm, v_hbm, g_hbm, placed, sums, chosen,
-    state, m_buf, v_buf, g_buf, squares, member, begins, ends, part, tail, head, left_rim, right_rim,
+    state, m_buf, v_buf, g_buf, member, part, tail, head, left_rim, right_rim,
     before, after, slots, old_ref, new_ref, seg_ref, sems, table_sems, send, receive, rim_send, rim_receive,
 ):
     rows = m_buf.shape[0]
     blocks = rows // BLOCK
-    segs = seg_ref.shape[0]
+    segs = seg_ref.shape[1]
     me = lax.axis_index(axis)
     right = lax.rem(me + 1, n)
     left = lax.rem(me + n - 1, n)
     tables = fetched((old_hbm, new_hbm, seg_hbm), (old_ref, new_ref, seg_ref), table_sems)
-    step_blocks = -(-blocks // sems.shape[1])
-    chunks = [(b, min(b + step_blocks, blocks)) for b in range(0, blocks, step_blocks)]
-    copies = []
-    for c, (b0, b1) in enumerate(chunks):
-        window = pl.ds(b0 * BLOCK, (b1 - b0) * BLOCK)
-        inside = state.at[0, pl.ds(PAD + b0 * BLOCK, (b1 - b0) * BLOCK)]
+    middle = -(-rows // (2 * TILE)) * TILE
+    halves = []
+    for c, (r0, r1) in enumerate(((0, middle), (middle, rows))):
+        window = pl.ds(r0, r1 - r0)
         group = [
-            pltpu.make_async_copy(w_hbm.at[window], inside, sems.at[0, c]),
+            pltpu.make_async_copy(g_hbm.at[window], g_buf.at[window], sems.at[3, c]),
             pltpu.make_async_copy(m_hbm.at[window], m_buf.at[window], sems.at[1, c]),
             pltpu.make_async_copy(v_hbm.at[window], v_buf.at[window], sems.at[2, c]),
-            pltpu.make_async_copy(g_hbm.at[window], g_buf.at[window], sems.at[3, c]),
+            pltpu.make_async_copy(w_hbm.at[window], state.at[0, pl.ds(PAD + r0, r1 - r0)], sems.at[0, c]),
         ]
         for copy in group:
             copy.start()
-        copies.append(group)
+        halves.append(group)
 
     barrier = pltpu.get_barrier_semaphore()
 
@@ -93,23 +92,20 @@
     new_count = new_ref[me + 1] - new_low
     shift = new_low - low
     phase = (-low) & (HALF - 1)
-
-    def bound_all(origin, offset):
-        def bound(s, carry):
-            value = (seg_ref[s] - origin - offset) >> HALF_BITS
-            begins[pl.ds(s, 1), :] = jnp.full((1, LANES), value, jnp.int32)
-            following = (seg_ref[jnp.minimum(s + 1, segs - 1)] - origin - offset) >> HALF_BITS
-            following = jnp.where(s + 1 < segs, following, 4 * rows)
-            ends[pl.ds(s, 1), :] = jnp.full((1, LANES), following, jnp.int32)
-            return carry
-
-        lax.fori_loop(0, segs, bound, 0, unroll=8)
-
-    bound_all(low, phase)
+    spot = lane_ids(segs)
+    line = lax.broadcasted_iota(jnp.int32, (segs, LANES), 0)
+    square_line = lax.broadcasted_iota(jnp.int32, (segs, segs), 0)
+    square_spot = lax.broadcasted_iota(jnp.int32, (segs, segs), 1)
+    starts = (seg_ref[...] >> HALF_BITS).astype(jnp.float32)
+    first = jnp.sum(jnp.where(square_spot == square_line, starts, 0.0), axis=1, keepdims=True)
+    past = jnp.sum(jnp.where(square_spot == square_line + 1, starts, 0.0), axis=1, keepdims=True)
+    past = jnp.where(square_line[:, :1] == segs - 1, 4.0 * n * rows, past)
+    first = jnp.broadcast_to(first.astype(jnp.int32), (segs, LANES))
+    past = jnp.broadcast_to(past.astype(jnp.int32), (segs, LANES))
+    base = (low + phase) >> HALF_BITS
+    first_half = first - base
+    past_half = past - base
     padded = member.shape[1]
-    spot = lane_ids(segs)
-    first_half = begins[...]
-    past_half = ends[...]
     for group in range(3):
         for tile in range(padded // LANES):
             half = 2 * (spot + tile * LANES) - 1 + group
@@ -117,50 +113,49 @@
             member[group * segs : (group + 1) * segs, tile * LANES : (tile + 1) * LANES] = jnp.where(
                 mask, 1.0, 0.0
             ).astype(jnp.bfloat16)
-    squares[rows:padded, :] = jnp.zeros((padded - rows, 4 * LANES), jnp.bfloat16)
 
     flat = flat_ids()
 
-    def advance(b, carry):
-        here = pl.multiple_of(b * BLOCK, BLOCK)
-        there = pl.multiple_of(b * BLOCK + PAD, 8)
-        gradient = g_buf[pl.ds(here, BLOCK), :].astype(jnp.float32)
-        weight = state[0, pl.ds(there, BLOCK), :]
-        moment = BETA_ONE * m_buf[pl.ds(here, BLOCK), :] + (1.0 - BETA_ONE) * gradient
-        second = BETA_TWO * v_buf[pl.ds(here, BLOCK), :] + (1.0 - BETA_TWO) * gradient * gradient
-        scaled = moment * (1.0 / CORR_ONE)
-        update = scaled / (jnp.sqrt(second * (1.0 / CORR_TWO)) + EPSILON) + DECAY * weight
-        state[1, pl.ds(there, BLOCK), :] = update
-        state[2, pl.ds(there, BLOCK), :] = moment
-        state[3, pl.ds(there, BLOCK), :] = second
-        live = flat + b * MARGIN < count
-        for i, value in enumerate((weight, update)):
-            square = jnp.where(live, value * value, 0.0)
-            coarse = square.astype(jnp.bfloat16)
-            fine = (square - coarse.astype(jnp.float32)).astype(jnp.bfloat16)
-            squares[pl.ds(here, BLOCK), i * LANES : (i + 1) * LANES] = coarse
-            squares[pl.ds(here, BLOCK), (i + 2) * LANES : (i + 3) * LANES] = fine
-        return carry
-
-    for (b0, b1), group in zip(chunks, copies):
-        for copy in group:
-            copy.wait()
-        lax.fori_loop(b0, b1, advance, 0, unroll=2)
-
-    start = count - MARGIN
-    start_row = start >> LANE_BITS
-    start_lane = start & (LANES - 1)
-    for a in range(4):
-        head[a] = state[a, PAD : PAD + BLOCK, :]
-        tail[a] = moved(
-            state[a, pl.ds(PAD + start_row, BLOCK), :],
-            state[a, pl.ds(PAD + start_row + 1, BLOCK), :],
-            start_lane,
-        )
-
-    product = jnp.dot(member[...], squares[...], preferred_element_type=jnp.float32)
+    def advance(r0):
+        here = slice(r0, r0 + BLOCK)
+        there = slice(r0 + PAD, r0 + PAD + BLOCK)
+        gradient = g_buf[here, :].astype(jnp.float32)
+        weight = state[0, there, :]
+        moment = BETA_ONE * m_buf[here, :] + (1.0 - BETA_ONE) * gradient
+        second = BETA_TWO * v_buf[here, :] + ((1.0 - BETA_TWO) * gradient) * gradient
+        spread = second * (CORR_ONE * CORR_ONE / CORR_TWO)
+        update = moment / (spread * lax.rsqrt(spread) + CORR_ONE * EPSILON) + DECAY * weight
+        state[1, there, :] = update
+        state[2, there, :] = moment
+        state[3, there, :] = second
+        return weight, update
+
+    for copy in halves[0]:
+        copy.wait()
+    for r0 in range(0, middle, BLOCK):
+        advance(r0)
+    for copy in halves[1]:
+        copy.wait()
+    product = None
+    for t0 in range(0, rows, TILE):
+        t1 = min(t0 + TILE, rows)
+        pieces = [[], [], [], []]
+        for r0 in range(t0, t1, BLOCK):
+            if r0 < middle:
+                values = [state[a, r0 + PAD : r0 + PAD + BLOCK, :] for a in range(2)]
+            else:
+                values = advance(r0)
+            for i, value in enumerate(values):
+                square = value * value
+                if r0 + 2 * BLOCK >= rows:
+                    square = jnp.where(flat + r0 * LANES < count, square, 0.0)
+                coarse = square.astype(jnp.bfloat16)
+                pieces[i].append(coarse)
+                pieces[i + 2].append((square - coarse.astype(jnp.float32)).astype(jnp.bfloat16))
+        squares = jnp.concatenate([jnp.concatenate(p, axis=0) for p in pieces], axis=1)
+        partial = jnp.dot(member[:, t0:t1], squares, preferred_element_type=jnp.float32)
+        product = partial if product is None else product + partial
     product = product[:, : 2 * LANES] + product[:, 2 * LANES :]
-    line = lax.broadcasted_iota(jnp.int32, (segs, LANES), 0)
     row = jnp.zeros((segs, LANES), jnp.float32)
     for i in range(2):
         columns = slice(i * LANES, (i + 1) * LANES)
@@ -206,6 +201,17 @@
         tell(k).start()
     pltpu.make_async_copy(part, slots.at[me], receive).start()
 
+    start = count - MARGIN
+    start_row = start >> LANE_BITS
+    start_lane = start & (LANES - 1)
+    for a in range(4):
+        head[a] = state[a, PAD : PAD + BLOCK, :]
+        tail[a] = moved(
+            state[a, pl.ds(PAD + start_row, BLOCK), :],
+            state[a, pl.ds(PAD + start_row + 1, BLOCK), :],
+            start_lane,
+        )
+
     @pl.when(me < n - 1)
     def send_tail():
         onward.start()
@@ -230,6 +236,27 @@
     lax.fori_loop(1, blocks - 3, inner, 0, unroll=3)
     for a in range(4):
         before[a, BLOCK:EDGE, :] = state[a, PAD : PAD + EDGE - BLOCK, :]
+
+    new_phase = (-new_low) & (HALF - 1)
+    new_base = (new_low + new_phase) >> HALF_BITS
+    on_lane = (spot & (segs - 1)) == line
+    lows = jnp.sum(jnp.where(on_lane, first - new_base, 0), axis=0, keepdims=True)
+    highs = jnp.sum(jnp.where(on_lane, past - new_base, 0), axis=0, keepdims=True)
+    block_row = lax.broadcasted_iota(jnp.int32, (BLOCK, LANES), 0)
+    lane_group = lane_ids() >> HALF_BITS
+
+    def choose(b, carry):
+        here = pl.multiple_of(b * BLOCK, BLOCK)
+        for tile in range(2):
+            half = 2 * (block_row + b * BLOCK) - 1 + 2 * tile + lane_group
+            mask = (half >= lows) & (half < highs)
+            chosen[pl.ds(here, BLOCK), tile * LANES : (tile + 1) * LANES] = jnp.where(mask, 1.0, 0.0).astype(
+                jnp.bfloat16
+            )
+        return carry
+
+    lax.fori_loop(0, blocks, choose, 0, unroll=2)
+    sums[1:2, :] = jnp.full((1, LANES), new_phase, jnp.int32).astype(jnp.float32)
 
     @pl.when(me < n - 1)
     def end_right():
@@ -260,27 +287,6 @@
             rim = moved(after[a, pl.ds(near, BLOCK), :], after[a, pl.ds(near + 1, BLOCK), :], side)
             value = jnp.where(beyond, rim, own(a, b))
             placed[a, b * BLOCK : (b + 1) * BLOCK, :] = jnp.where(live, value, 0.0)
-
-    new_phase = (-new_low) & (HALF - 1)
-    bound_all(new_low, new_phase)
-    on_lane = (spot & (segs - 1)) == line
-    lows = jnp.sum(jnp.where(on_lane, begins[...], 0), axis=0, keepdims=True)
-    highs = jnp.sum(jnp.where(on_lane, ends[...], 0), axis=0, keepdims=True)
-    block_row = lax.broadcasted_iota(jnp.int32, (BLOCK, LANES), 0)
-    lane_group = lane_ids() >> HALF_BITS
-
-    def choose(b, carry):
-        here = pl.multiple_of(b * BLOCK, BLOCK)
-        for tile in range(2):
-            half = 2 * (block_row + b * BLOCK) - 1 + 2 * tile + lane_group
-            mask = (half >= lows) & (half < highs)
-            chosen[pl.ds(here, BLOCK), tile * LANES : (tile + 1) * LANES] = jnp.where(mask, 1.0, 0.0).astype(
-                jnp.bfloat16
-            )
-        return carry
-
-    lax.fori_loop(0, blocks, choose, 0, unroll=2)
-    sums[1:2, :] = jnp.full((1, LANES), new_phase, jnp.int32).astype(jnp.float32)
 
     pltpu.make_async_copy(slots, slots, receive).wait()
     sums[0:1, :] = jnp.sum(slots[...], axis=0)
@@ -341,14 +347,15 @@
     rows = cap // LANES
     f32 = jnp.float32
     flat = [x.reshape(rows, LANES) for x in (params, first_moment, second_moment, grads)]
-    old_bounds, new_bounds, seg_start, *flat = (
-        pltpu.with_memory_space_constraint(x, pltpu.HBM) for x in (old_bounds, new_bounds, seg_start, *flat)
+    segs = seg_start.shape[0]
+    tables = (old_bounds, new_bounds, seg_start.reshape(1, segs))
+    old_bounds, new_bounds, starts_row, *flat = (
+        pltpu.with_memory_space_constraint(x, pltpu.HBM) for x in (*tables, *flat)
     )
-    segs = seg_start.shape[0]
-    padded = -(-rows // 256) * 256
+    padded = -(-rows // LANES) * LANES
     vmem, hbm = spec(pltpu.VMEM), spec(pltpu.HBM)
     bounds = pltpu.SMEM(old_bounds.shape, jnp.int32)
-    starts = pltpu.SMEM(seg_start.shape, jnp.int32)
+    starts = pltpu.VMEM((1, segs), jnp.int32)
     rim = pltpu.VMEM((4, BLOCK, LANES), f32)
     dma = pltpu.SemaphoreType.DMA
     placed, sums, chosen = pl.pallas_call(
@@ -366,10 +373,7 @@
             pltpu.VMEM((rows, LANES), f32),
             pltpu.VMEM((rows, LANES), f32),
             pltpu.VMEM((rows, LANES), grads.dtype),
-            pltpu.VMEM((padded, 4 * LANES), jnp.bfloat16),
             pltpu.VMEM((3 * segs, padded), jnp.bfloat16),
-            pltpu.VMEM((segs, LANES), jnp.int32),
-            pltpu.VMEM((segs, LANES), jnp.int32),
             pltpu.VMEM((1, LANES), f32),
             rim,
             rim,
@@ -391,7 +395,7 @@
         compiler_params=pltpu.CompilerParams(
             collective_id=0, has_side_effects=True, vmem_limit_bytes=VMEM_LIMIT
         ),
-    )(old_bounds, new_bounds, seg_start, *flat)
+    )(old_bounds, new_bounds, starts_row, *flat)
     whole = jax.ShapeDtypeStruct((rows, LANES), f32)
     outs = pl.pallas_call(
         functools.partial(apply_kernel, segs),

time: 13.3 us -> 12.8 us (0.962)
  Pallas kernels: 12.5 us -> 12.1 us
    pallas_call x1, Pallas kernels: 11.2 us -> 10.8 us  [shards(): pl.pallas_call(functools.partial(step_kernel, axis, n), name='step', out_...]
where the time goes in v2:
time: 12.8 us; the launch traced here: 12.7 us
  Pallas kernels  12.1 us (95%)
  between operations  0.64 us (5%)
    pallas_call x1, Pallas kernels, shards(): pl.pallas_call(functools.partial(step_kernel, axis, n), name='step', out_...  10.8 us
    pallas_call x1, Pallas kernels, shards(): pl.pallas_call(functools.partial(apply_kernel, segs), name='apply', out_s...  1.24 us

profile of v2, /device:TPU:0, one launch (start us, length us, event | category | flops | bytes accessed | tf_op | source)
XLA Modules:
  0.0 12.7 jit_solution(16111874829780621467)
XLA Ops:
  0.6 10.8 %step.1 = (f32[4,992,128]{2,1,0:T(8,128)S(1)}, f32[2,128]{1,0:T(2,128)S(1)}, bf16[992,256]{1,0:T(8,128)(2,1)S(1)}) custom-call(s32[33]{0:T(128)} %old_hbm.1, s32[33]{0:T(128)} %new_hbm.1, s32[1,64]{1,0:T(1,128)} %bitcast.12, f32[992,128]{1,0:T(8,128)} %bitcast.8, f32[992,128]{1,0:T(8,128)} %bitcast.9, f32[992,128]{1,0:T(8,128)} %bitcast.10, ...), custom_call_target="tpu_custom_call" | custom-call | tf_op jit(solution)/shard_map/step/pallas_call | solution.py:361
  11.5 1.2 %apply.1 = (f32[992,128]{1,0:T(8,128)}, f32[992,128]{1,0:T(8,128)}, f32[992,128]{1,0:T(8,128)}) custom-call(f32[4,992,128]{2,1,0:T(8,128)S(1)} %get-tuple-element.9.placed, f32[2,128]{1,0:T(2,128)S(1)} %get-tuple-element.10.sums, bf16[992,256]{1,0:T(8,128)(2,1)S(1)} %get-tuple-element.11.chosen), custom_call_target="tpu_custom_call" | custom-call | tf_op jit(solution)/shard_map/apply/pallas_call | solution.py:400

commit v3 on v2

--- a/solution.py
+++ b/solution.py
@@ -16,6 +16,7 @@
 PAD = BLOCK + 8
 EDGE = 2 * PAD + BLOCK
 TILE = 256
+REACH = 4
 
 
 BETA_ONE = 0.9
@@ -51,9 +52,9 @@
 
 
 def step_kernel(
-    axis, n, old_hbm, new_hbm, seg_hbm, w_hbm, m_hbm, v_hbm, g_hbm, placed, sums, chosen,
+    axis, n, old_hbm, new_hbm, seg_hbm, w_hbm, m_hbm, v_hbm, g_hbm, placed, sums, chosen, wide,
     state, m_buf, v_buf, g_buf, member, part, tail, head, left_rim, right_rim,
-    before, after, slots, old_ref, new_ref, seg_ref, sems, table_sems, send, receive, rim_send, rim_receive,
+    before, after, slots, old_ref, new_ref, seg_ref, seg_list, sems, table_sems, send, receive, rim_send, rim_receive,
 ):
     rows = m_buf.shape[0]
     blocks = rows // BLOCK
@@ -61,28 +62,20 @@
     me = lax.axis_index(axis)
     right = lax.rem(me + 1, n)
     left = lax.rem(me + n - 1, n)
-    tables = fetched((old_hbm, new_hbm, seg_hbm), (old_ref, new_ref, seg_ref), table_sems)
-    middle = -(-rows // (2 * TILE)) * TILE
-    halves = []
-    for c, (r0, r1) in enumerate(((0, middle), (middle, rows))):
-        window = pl.ds(r0, r1 - r0)
-        group = [
-            pltpu.make_async_copy(g_hbm.at[window], g_buf.at[window], sems.at[3, c]),
-            pltpu.make_async_copy(m_hbm.at[window], m_buf.at[window], sems.at[1, c]),
-            pltpu.make_async_copy(v_hbm.at[window], v_buf.at[window], sems.at[2, c]),
-            pltpu.make_async_copy(w_hbm.at[window], state.at[0, pl.ds(PAD + r0, r1 - r0)], sems.at[0, c]),
-        ]
-        for copy in group:
-            copy.start()
-        halves.append(group)
-
+    tables = fetched((old_hbm, new_hbm, seg_hbm, seg_hbm), (old_ref, new_ref, seg_ref, seg_list), table_sems)
+    weights = state.at[0, pl.ds(PAD, rows)]
+    loads = fetched((g_hbm, m_hbm, v_hbm, w_hbm), (g_buf, m_buf, v_buf, weights), sems)
     barrier = pltpu.get_barrier_semaphore()
-
-    def greet(k, carry):
-        pl.semaphore_signal(barrier, inc=1, device_id=(lax.rem(me + k, n),), device_id_type=MESH)
-        return carry
-
-    lax.fori_loop(1, n, greet, 0)
+    near = [k for k in range(-REACH, REACH + 1) if k and abs(k) < n]
+
+    def inside(k):
+        return (me + k >= 0) & (me + k < n)
+
+    for k in near:
+
+        @pl.when(inside(k))
+        def greet(k=k):
+            pl.semaphore_signal(barrier, inc=1, device_id=(me + k,), device_id_type=MESH)
 
     for copy in tables:
         copy.wait()
@@ -116,36 +109,29 @@
 
     flat = flat_ids()
 
-    def advance(r0):
+    for copy in loads[:3]:
+        copy.wait()
+    for r0 in range(0, rows, BLOCK):
         here = slice(r0, r0 + BLOCK)
         there = slice(r0 + PAD, r0 + PAD + BLOCK)
         gradient = g_buf[here, :].astype(jnp.float32)
-        weight = state[0, there, :]
         moment = BETA_ONE * m_buf[here, :] + (1.0 - BETA_ONE) * gradient
         second = BETA_TWO * v_buf[here, :] + ((1.0 - BETA_TWO) * gradient) * gradient
         spread = second * (CORR_ONE * CORR_ONE / CORR_TWO)
-        update = moment / (spread * lax.rsqrt(spread) + CORR_ONE * EPSILON) + DECAY * weight
-        state[1, there, :] = update
+        state[1, there, :] = moment / (spread * lax.rsqrt(spread) + CORR_ONE * EPSILON)
         state[2, there, :] = moment
         state[3, there, :] = second
-        return weight, update
-
-    for copy in halves[0]:
-        copy.wait()
-    for r0 in range(0, middle, BLOCK):
-        advance(r0)
-    for copy in halves[1]:
-        copy.wait()
+    loads[3].wait()
     product = None
     for t0 in range(0, rows, TILE):
         t1 = min(t0 + TILE, rows)
         pieces = [[], [], [], []]
         for r0 in range(t0, t1, BLOCK):
-            if r0 < middle:
-                values = [state[a, r0 + PAD : r0 + PAD + BLOCK, :] for a in range(2)]
-            else:
-                values = advance(r0)
-            for i, value in enumerate(values):
+            there = slice(r0 + PAD, r0 + PAD + BLOCK)
+            weight = state[0, there, :]
+            update = state[1, there, :] + DECAY * weight
+            state[1, there, :] = update
+            for i, value in enumerate((weight, update)):
                 square = value * value
                 if r0 + 2 * BLOCK >= rows:
                     square = jnp.where(flat + r0 * LANES < count, square, 0.0)
@@ -156,7 +142,7 @@
         partial = jnp.dot(member[:, t0:t1], squares, preferred_element_type=jnp.float32)
         product = partial if product is None else product + partial
     product = product[:, : 2 * LANES] + product[:, 2 * LANES :]
-    row = jnp.zeros((segs, LANES), jnp.float32)
+    on_lane = (spot & (segs - 1)) == line
     for i in range(2):
         columns = slice(i * LANES, (i + 1) * LANES)
         mixed = jnp.where(
@@ -166,17 +152,17 @@
                 spot < phase + HALF, product[segs : 2 * segs, columns], product[2 * segs : 3 * segs, columns]
             ),
         )
-        row = jnp.where(spot == line + i * segs, jnp.sum(mixed, axis=1, keepdims=True), row)
-    part[...] = jnp.sum(row, axis=0, keepdims=True)
-    pl.semaphore_wait(barrier, n - 1)
+        column = jnp.sum(mixed, axis=1, keepdims=True)
+        part[i : i + 1, :] = jnp.sum(jnp.where(on_lane, column, 0.0), axis=0, keepdims=True)
+    pl.semaphore_wait(barrier, jnp.minimum(me, REACH) + jnp.minimum(n - 1 - me, REACH))
 
     def tell(k):
         return pltpu.make_async_remote_copy(
             src_ref=part,
-            dst_ref=slots.at[me],
-            send_sem=send,
-            recv_sem=receive,
-            device_id=(lax.rem(me + k, n),),
+            dst_ref=slots.at[k + REACH],
+            send_sem=send.at[k + REACH],
+            recv_sem=receive.at[k + REACH],
+            device_id=(me + k,),
             device_id_type=MESH,
         )
 
@@ -197,9 +183,13 @@
         device_id_type=MESH,
     )
 
-    for k in range(1, n):
-        tell(k).start()
-    pltpu.make_async_copy(part, slots.at[me], receive).start()
+    for k in near:
+
+        @pl.when(inside(k))
+        def send_sums(k=k):
+            tell(k).start()
+
+    sums[3:5, :] = part[...]
 
     start = count - MARGIN
     start_row = start >> LANE_BITS
@@ -239,7 +229,6 @@
 
     new_phase = (-new_low) & (HALF - 1)
     new_base = (new_low + new_phase) >> HALF_BITS
-    on_lane = (spot & (segs - 1)) == line
     lows = jnp.sum(jnp.where(on_lane, first - new_base, 0), axis=0, keepdims=True)
     highs = jnp.sum(jnp.where(on_lane, past - new_base, 0), axis=0, keepdims=True)
     block_row = lax.broadcasted_iota(jnp.int32, (BLOCK, LANES), 0)
@@ -256,7 +245,13 @@
         return carry
 
     lax.fori_loop(0, blocks, choose, 0, unroll=2)
-    sums[1:2, :] = jnp.full((1, LANES), new_phase, jnp.int32).astype(jnp.float32)
+    sums[2:3, :] = jnp.full((1, LANES), new_phase, jnp.int32).astype(jnp.float32)
+
+    def longest(s, most):
+        return jnp.maximum(most, seg_list[0, s + 1] - seg_list[0, s])
+
+    most = lax.fori_loop(0, segs - 1, longest, old_ref[n] - seg_list[0, segs - 1], unroll=9)
+    wide[0] = jnp.where(most > REACH * (rows * LANES - 2 * MARGIN) - MARGIN, 1, 0)
 
     @pl.when(me < n - 1)
     def end_right():
@@ -278,18 +273,60 @@
 
     for b in range(blocks - 3, blocks):
         offset = b * MARGIN + shift - count
-        near = jnp.clip(offset >> LANE_BITS, -PAD, PAD - 7) + PAD
+        edge = jnp.clip(offset >> LANE_BITS, -PAD, PAD - 7) + PAD
         side = offset & (LANES - 1)
         index = flat + b * MARGIN
         beyond = index + shift >= count
         live = index < new_count
         for a in range(4):
-            rim = moved(after[a, pl.ds(near, BLOCK), :], after[a, pl.ds(near + 1, BLOCK), :], side)
+            rim = moved(after[a, pl.ds(edge, BLOCK), :], after[a, pl.ds(edge + 1, BLOCK), :], side)
             value = jnp.where(beyond, rim, own(a, b))
             placed[a, b * BLOCK : (b + 1) * BLOCK, :] = jnp.where(live, value, 0.0)
 
+    total = part[...]
+    for k in near:
+
+        @pl.when(inside(-k))
+        def get_sums(k=k):
+            tell(k).wait_recv()
+
+        total = total + jnp.where(inside(-k), slots[k + REACH], 0.0)
+    sums[0:2, :] = total
+    for k in near:
+
+        @pl.when(inside(k))
+        def end_sums(k=k):
+            tell(k).wait_send()
+
+
+def everyone_kernel(axis, n, near_sums, sums, part, slots, send, receive):
+    me = lax.axis_index(axis)
+    barrier = pltpu.get_barrier_semaphore()
+
+    def greet(k, carry):
+        pl.semaphore_signal(barrier, inc=1, device_id=(lax.rem(me + k, n),), device_id_type=MESH)
+        return carry
+
+    lax.fori_loop(1, n, greet, 0)
+    part[...] = near_sums[3:5, :]
+    sums[2:5, :] = near_sums[2:5, :]
+    pl.semaphore_wait(barrier, n - 1)
+
+    def tell(k, carry):
+        pltpu.make_async_remote_copy(
+            src_ref=part,
+            dst_ref=slots.at[me],
+            send_sem=send,
+            recv_sem=receive,
+            device_id=(lax.rem(me + k, n),),
+            device_id_type=MESH,
+        ).start()
+        return carry
+
+    lax.fori_loop(1, n, tell, 0)
+    pltpu.make_async_copy(part, slots.at[me], receive).start()
     pltpu.make_async_copy(slots, slots, receive).wait()
-    sums[0:1, :] = jnp.sum(slots[...], axis=0)
+    sums[0:2, :] = jnp.sum(slots[...], axis=0)
     others = slots.at[pl.ds(0, n - 1)]
     pltpu.make_async_copy(others, others, send).wait()
 
@@ -301,33 +338,30 @@
     v_copy.start()
     rows = w_buf.shape[0]
     total = sums[0:1, :]
-    phase = sums[1:2, :]
-    other = pltpu.roll(total, LANES - segs, 1)
+    other = sums[1:2, :]
+    phase = sums[2:3, :]
     rate = LEARN * (jnp.sqrt(total) / (jnp.sqrt(other) + EPSILON))
-    spot = lane_ids(segs)
-    line = lax.broadcasted_iota(jnp.int32, (segs, LANES), 0)
-    column = jnp.sum(jnp.where(spot == line, rate, 0.0), axis=1, keepdims=True)
-    place = spot.astype(jnp.float32)
+    place = lax.broadcasted_iota(jnp.int32, (LANES, LANES), 0).astype(jnp.float32)
+    lower = lane_ids(LANES) < segs
     early = place < phase
     late = place >= phase + HALF
-    nothing = jnp.zeros((segs, LANES), jnp.float32)
     rates = jnp.concatenate(
         [
-            jnp.where(early, column, 0.0),
-            jnp.where(early | late, 0.0, column),
-            jnp.where(late, column, 0.0),
-            nothing,
+            jnp.where((lower & early) | ~(lower | early | late), rate, 0.0),
+            jnp.where(lower & late, rate, 0.0),
         ],
-        axis=0,
+        axis=1,
     )
     coarse = rates.astype(jnp.bfloat16)
     fine = (rates - coarse.astype(jnp.float32)).astype(jnp.bfloat16)
-    table = jnp.concatenate([coarse, fine], axis=1)
+    table = jnp.concatenate([coarse, fine], axis=0)
     step = 256
     copies = []
     for c, r0 in enumerate(range(0, rows, step)):
         size = min(step, rows - r0)
-        product = jnp.dot(chosen[r0 : r0 + size, :], table, preferred_element_type=jnp.float32)
+        product = lax.dot_general(
+            chosen[r0 : r0 + size, :], table, (((1,), (1,)), ((), ())), preferred_element_type=jnp.float32
+        )
         factor = product[:, :LANES] + product[:, LANES:]
         w_buf[r0 : r0 + size, :] = placed[0, r0 : r0 + size, :] - factor * placed[1, r0 : r0 + size, :]
         window = pl.ds(r0, size)
@@ -358,37 +392,39 @@
     starts = pltpu.VMEM((1, segs), jnp.int32)
     rim = pltpu.VMEM((4, BLOCK, LANES), f32)
     dma = pltpu.SemaphoreType.DMA
-    placed, sums, chosen = pl.pallas_call(
+    placed, sums, chosen, wide = pl.pallas_call(
         functools.partial(step_kernel, axis, n),
         name="step",
         out_shape=(
             jax.ShapeDtypeStruct((4, rows, LANES), f32),
-            jax.ShapeDtypeStruct((2, LANES), f32),
+            jax.ShapeDtypeStruct((5, LANES), f32),
             jax.ShapeDtypeStruct((rows, 2 * LANES), jnp.bfloat16),
+            jax.ShapeDtypeStruct((1,), jnp.int32),
         ),
         in_specs=[hbm] * 7,
-        out_specs=(vmem,) * 3,
+        out_specs=(vmem, vmem, vmem, spec(pltpu.SMEM)),
         scratch_shapes=[
             pltpu.VMEM((4, rows + 2 * PAD, LANES), f32),
             pltpu.VMEM((rows, LANES), f32),
             pltpu.VMEM((rows, LANES), f32),
             pltpu.VMEM((rows, LANES), grads.dtype),
             pltpu.VMEM((3 * segs, padded), jnp.bfloat16),
-            pltpu.VMEM((1, LANES), f32),
+            pltpu.VMEM((2, LANES), f32),
             rim,
             rim,
             rim,
             rim,
             pltpu.VMEM((4, EDGE, LANES), f32),
             pltpu.VMEM((4, EDGE, LANES), f32),
-            pltpu.VMEM((n, 1, LANES), f32),
+            pltpu.VMEM((2 * REACH + 1, 2, LANES), f32),
             bounds,
             bounds,
             starts,
-            dma((4, 2)),
-            dma((3,)),
-            dma,
-            dma,
+            pltpu.SMEM((1, segs), jnp.int32),
+            dma((4,)),
+            dma((4,)),
+            dma((2 * REACH + 1,)),
+            dma((2 * REACH + 1,)),
             dma((2,)),
             dma((2,)),
         ],
@@ -397,15 +433,32 @@
         ),
     )(old_bounds, new_bounds, starts_row, *flat)
     whole = jax.ShapeDtypeStruct((rows, LANES), f32)
-    outs = pl.pallas_call(
-        functools.partial(apply_kernel, segs),
-        name="apply",
-        out_shape=(whole,) * 3,
-        in_specs=[vmem] * 3,
-        out_specs=(hbm,) * 3,
-        scratch_shapes=[pltpu.VMEM((rows, LANES), f32), dma((2 + -(-rows // 256),))],
-        compiler_params=pltpu.CompilerParams(vmem_limit_bytes=VMEM_LIMIT),
-    )(placed, sums, chosen)
+    def finish(placed, sums, chosen):
+        return pl.pallas_call(
+            functools.partial(apply_kernel, segs),
+            name="apply",
+            out_shape=(whole,) * 3,
+            in_specs=[vmem] * 3,
+            out_specs=(hbm,) * 3,
+            scratch_shapes=[pltpu.VMEM((rows, LANES), f32), dma((2 + -(-rows // 256),))],
+            compiler_params=pltpu.CompilerParams(vmem_limit_bytes=VMEM_LIMIT),
+        )(placed, sums, chosen)
+
+    def gather(placed, sums, chosen):
+        sums = pl.pallas_call(
+            functools.partial(everyone_kernel, axis, n),
+            name="everyone",
+            out_shape=jax.ShapeDtypeStruct((5, LANES), f32),
+            in_specs=[vmem],
+            out_specs=vmem,
+            scratch_shapes=[pltpu.VMEM((2, LANES), f32), pltpu.VMEM((n, 2, LANES), f32), dma, dma],
+            compiler_params=pltpu.CompilerParams(
+                collective_id=1, has_side_effects=True, vmem_limit_bytes=VMEM_LIMIT
+            ),
+        )(sums)
+        return finish(placed, sums, chosen)
+
+    outs = lax.switch(wide.reshape(()), (finish, gather), placed, sums, chosen)
     return tuple(x.reshape(cap) for x in outs)
 
 

time: 12.8 us -> 10.4 us (0.81)
  the two profiles are of different devices: /device:TPU:0 before, /device:TPU:1 now
where the time goes in v3:
time: 10.4 us; the launch traced here: 10.2 us
  Pallas kernels  8.95 us (86%)
  between operations  1.26 us (12%)
    pallas_call x1, Pallas kernels, shards(): pl.pallas_call(functools.partial(step_kernel, axis, n), name='step', out_...  7.79 us
    pallas_call x1, Pallas kernels, finish(): pl.pallas_call(functools.partial(apply_kernel, segs), name='apply', out_s...  1.16 us

profile of v3, /device:TPU:1, one launch (start us, length us, event | category | flops | bytes accessed | tf_op | source)
XLA Modules:
  0.0 10.2 jit_solution(16188794143918378528)
XLA Ops:
  0.6 7.8 %step.1 = (f32[4,992,128]{2,1,0:T(8,128)S(1)}, f32[5,128]{1,0:T(8,128)S(1)}, bf16[992,256]{1,0:T(8,128)(2,1)S(1)}, s32[1]{0:T(128)}) custom-call(s32[33]{0:T(128)} %old_hbm.1, s32[33]{0:T(128)} %new_hbm.1, s32[1,64]{1,0:T(1,128)} %bitcast.13, f32[992,128]{1,0:T(8,128)} %bitcast.9, f32[992,128]{1,0:T(8,128)} %bitcast.10, f32[992,128]{1,0:T(8,128)} %bitcast.11, ...), custom_call_target="tpu_custom_call" | custom-call | tf_op jit(solution)/shard_map/step/pallas_call | solution.py:395
  9.0 1.2 %conditional.1 = ((f32[992,128]{1,0:T(8,128)}, f32[992,128]{1,0:T(8,128)}, f32[992,128]{1,0:T(8,128)})) conditional(s32[]{:T(128)} %bitcast.5, (f32[4,992,128]{2,1,0:T(8,128)S(1)}, f32[5,128]{1,0:T(8,128)S(1)}, bf16[992,256]{1,0:T(8,128)(2,1)S(1)}) %tuple.21, (f32[5,128]{1,0:T(8,128)S(1)}, f32[4,992,128]{2,1,0:T(8,128)S(1)}, ...), branch_computations={%region_0.0_spmd.clone, %region_1.0_spmd.clone} | conditional | bytes 8 | solution.py:461
  9.1 1.2 %apply.2 = (f32[992,128]{1,0:T(8,128)}, f32[992,128]{1,0:T(8,128)}, f32[992,128]{1,0:T(8,128)}) custom-call(f32[4,992,128]{2,1,0:T(8,128)S(1)} %get-tuple-element.49.placed, f32[5,128]{1,0:T(8,128)S(1)} %get-tuple-element.50.sums, bf16[992,256]{1,0:T(8,128)(2,1)S(1)} %get-tuple-element.51.chosen), custom_call_target="tpu_custom_call" | custom-call | tf_op jit(solution)/shard_map/cond/branch_0_fun/apply/pallas_call | solution.py:437

commit v4 on v3

--- a/solution.py
+++ b/solution.py
@@ -17,6 +17,7 @@
 EDGE = 2 * PAD + BLOCK
 TILE = 256
 REACH = 4
+UPDATE, WEIGHT, MOMENT, SECOND = range(4)
 
 
 BETA_ONE = 0.9
@@ -44,6 +45,11 @@
     return pltpu.roll(picked, (LANES - lanes) & (LANES - 1), 1)
 
 
+def adaptive(moment, second):
+    spread = second * (CORR_ONE * CORR_ONE / CORR_TWO)
+    return moment / (spread * lax.rsqrt(spread) + CORR_ONE * EPSILON)
+
+
 def fetched(tables, refs, sems):
     copies = [pltpu.make_async_copy(t, r, sems.at[i]) for i, (t, r) in enumerate(zip(tables, refs))]
     for copy in copies:
@@ -53,7 +59,7 @@
 
 def step_kernel(
     axis, n, old_hbm, new_hbm, seg_hbm, w_hbm, m_hbm, v_hbm, g_hbm, placed, sums, chosen, wide,
-    state, m_buf, v_buf, g_buf, member, part, tail, head, left_rim, right_rim,
+    state, m_buf, v_buf, g_buf, member, part, tail, left_rim, right_rim,
     before, after, slots, old_ref, new_ref, seg_ref, seg_list, sems, table_sems, send, receive, rim_send, rim_receive,
 ):
     rows = m_buf.shape[0]
@@ -63,7 +69,7 @@
     right = lax.rem(me + 1, n)
     left = lax.rem(me + n - 1, n)
     tables = fetched((old_hbm, new_hbm, seg_hbm, seg_hbm), (old_ref, new_ref, seg_ref, seg_list), table_sems)
-    weights = state.at[0, pl.ds(PAD, rows)]
+    weights = state.at[WEIGHT, pl.ds(PAD, rows)]
     loads = fetched((g_hbm, m_hbm, v_hbm, w_hbm), (g_buf, m_buf, v_buf, weights), sems)
     barrier = pltpu.get_barrier_semaphore()
     near = [k for k in range(-REACH, REACH + 1) if k and abs(k) < n]
@@ -117,20 +123,54 @@
         gradient = g_buf[here, :].astype(jnp.float32)
         moment = BETA_ONE * m_buf[here, :] + (1.0 - BETA_ONE) * gradient
         second = BETA_TWO * v_buf[here, :] + ((1.0 - BETA_TWO) * gradient) * gradient
-        spread = second * (CORR_ONE * CORR_ONE / CORR_TWO)
-        state[1, there, :] = moment / (spread * lax.rsqrt(spread) + CORR_ONE * EPSILON)
-        state[2, there, :] = moment
-        state[3, there, :] = second
+        state[UPDATE, there, :] = adaptive(moment, second)
+        state[MOMENT, there, :] = moment
+        state[SECOND, there, :] = second
     loads[3].wait()
+    pl.semaphore_wait(barrier, jnp.minimum(me, REACH) + jnp.minimum(n - 1 - me, REACH))
+    start = count - MARGIN
+    start_row = start >> LANE_BITS
+    start_lane = start & (LANES - 1)
+    for a in range(3):
+        tail[a] = moved(
+            state[a + 1, pl.ds(PAD + start_row, BLOCK), :],
+            state[a + 1, pl.ds(PAD + start_row + 1, BLOCK), :],
+            start_lane,
+        )
+    onward = pltpu.make_async_remote_copy(
+        src_ref=tail,
+        dst_ref=left_rim,
+        send_sem=rim_send.at[0],
+        recv_sem=rim_receive.at[0],
+        device_id=(right,),
+        device_id_type=MESH,
+    )
+    back = pltpu.make_async_remote_copy(
+        src_ref=state.at[pl.ds(1, 3), pl.ds(PAD, BLOCK)],
+        dst_ref=right_rim,
+        send_sem=rim_send.at[1],
+        recv_sem=rim_receive.at[1],
+        device_id=(left,),
+        device_id_type=MESH,
+    )
+
+    @pl.when(me < n - 1)
+    def send_tail():
+        onward.start()
+
+    @pl.when(me > 0)
+    def send_head():
+        back.start()
+
     product = None
     for t0 in range(0, rows, TILE):
         t1 = min(t0 + TILE, rows)
         pieces = [[], [], [], []]
         for r0 in range(t0, t1, BLOCK):
             there = slice(r0 + PAD, r0 + PAD + BLOCK)
-            weight = state[0, there, :]
-            update = state[1, there, :] + DECAY * weight
-            state[1, there, :] = update
+            weight = state[WEIGHT, there, :]
+            update = state[UPDATE, there, :] + DECAY * weight
+            state[UPDATE, there, :] = update
             for i, value in enumerate((weight, update)):
                 square = value * value
                 if r0 + 2 * BLOCK >= rows:
@@ -154,7 +194,6 @@
         )
         column = jnp.sum(mixed, axis=1, keepdims=True)
         part[i : i + 1, :] = jnp.sum(jnp.where(on_lane, column, 0.0), axis=0, keepdims=True)
-    pl.semaphore_wait(barrier, jnp.minimum(me, REACH) + jnp.minimum(n - 1 - me, REACH))
 
     def tell(k):
         return pltpu.make_async_remote_copy(
@@ -166,23 +205,6 @@
             device_id_type=MESH,
         )
 
-    onward = pltpu.make_async_remote_copy(
-        src_ref=tail,
-        dst_ref=left_rim,
-        send_sem=rim_send.at[0],
-        recv_sem=rim_receive.at[0],
-        device_id=(right,),
-        device_id_type=MESH,
-    )
-    back = pltpu.make_async_remote_copy(
-        src_ref=head,
-        dst_ref=right_rim,
-        send_sem=rim_send.at[1],
-        recv_sem=rim_receive.at[1],
-        device_id=(left,),
-        device_id_type=MESH,
-    )
-
     for k in near:
 
         @pl.when(inside(k))
@@ -190,25 +212,6 @@
             tell(k).start()
 
     sums[3:5, :] = part[...]
-
-    start = count - MARGIN
-    start_row = start >> LANE_BITS
-    start_lane = start & (LANES - 1)
-    for a in range(4):
-        head[a] = state[a, PAD : PAD + BLOCK, :]
-        tail[a] = moved(
-            state[a, pl.ds(PAD + start_row, BLOCK), :],
-            state[a, pl.ds(PAD + start_row + 1, BLOCK), :],
-            start_lane,
-        )
-
-    @pl.when(me < n - 1)
-    def send_tail():
-        onward.start()
-
-    @pl.when(me > 0)
-    def send_head():
-        back.start()
 
     top = shift >> LANE_BITS
     lanes = shift & (LANES - 1)
@@ -226,6 +229,10 @@
     lax.fori_loop(1, blocks - 3, inner, 0, unroll=3)
     for a in range(4):
         before[a, BLOCK:EDGE, :] = state[a, PAD : PAD + EDGE - BLOCK, :]
+    for b in range(blocks - 3, blocks):
+        live = flat + b * MARGIN < new_count
+        for a in range(4):
+            placed[a, b * BLOCK : (b + 1) * BLOCK, :] = jnp.where(live, own(a, b), 0.0)
 
     new_phase = (-new_low) & (HALF - 1)
     new_base = (new_low + new_phase) >> HALF_BITS
@@ -251,7 +258,7 @@
         return jnp.maximum(most, seg_list[0, s + 1] - seg_list[0, s])
 
     most = lax.fori_loop(0, segs - 1, longest, old_ref[n] - seg_list[0, segs - 1], unroll=9)
-    wide[0] = jnp.where(most > REACH * (rows * LANES - 2 * MARGIN) - MARGIN, 1, 0)
+    wide[...] = jnp.full((1, LANES), jnp.where(most > REACH * (rows * LANES - 2 * MARGIN) - MARGIN, 1, 0), jnp.int32)
 
     @pl.when(me < n - 1)
     def end_right():
@@ -263,9 +270,10 @@
         back.wait_send()
         onward.wait_recv()
 
-    for a in range(4):
-        before[a, 0:BLOCK, :] = left_rim[a]
-        after[a, PAD : PAD + BLOCK, :] = right_rim[a]
+    for ref, there, rim in ((before, slice(0, BLOCK), left_rim), (after, slice(PAD, PAD + BLOCK), right_rim)):
+        for a in range(3):
+            ref[a + 1, there, :] = rim[a]
+        ref[UPDATE, there, :] = adaptive(rim[1], rim[2]) + DECAY * rim[0]
     for a in range(4):
         placed[a, 0:BLOCK, :] = moved(
             before[a, pl.ds(BLOCK + top, BLOCK), :], before[a, pl.ds(BLOCK + top + 1, BLOCK), :], lanes
@@ -276,12 +284,11 @@
         edge = jnp.clip(offset >> LANE_BITS, -PAD, PAD - 7) + PAD
         side = offset & (LANES - 1)
         index = flat + b * MARGIN
-        beyond = index + shift >= count
-        live = index < new_count
+        beyond = (index + shift >= count) & (index < new_count)
+        here = slice(b * BLOCK, (b + 1) * BLOCK)
         for a in range(4):
             rim = moved(after[a, pl.ds(edge, BLOCK), :], after[a, pl.ds(edge + 1, BLOCK), :], side)
-            value = jnp.where(beyond, rim, own(a, b))
-            placed[a, b * BLOCK : (b + 1) * BLOCK, :] = jnp.where(live, value, 0.0)
+            placed[a, here, :] = jnp.where(beyond, rim, placed[a, here, :])
 
     total = part[...]
     for k in near:
@@ -332,8 +339,8 @@
 
 
 def apply_kernel(segs, placed, sums, chosen, w_out, m_out, v_out, w_buf, sems):
-    m_copy = pltpu.make_async_copy(placed.at[2], m_out, sems.at[0])
-    v_copy = pltpu.make_async_copy(placed.at[3], v_out, sems.at[1])
+    m_copy = pltpu.make_async_copy(placed.at[MOMENT], m_out, sems.at[0])
+    v_copy = pltpu.make_async_copy(placed.at[SECOND], v_out, sems.at[1])
     m_copy.start()
     v_copy.start()
     rows = w_buf.shape[0]
@@ -363,7 +370,7 @@
             chosen[r0 : r0 + size, :], table, (((1,), (1,)), ((), ())), preferred_element_type=jnp.float32
         )
         factor = product[:, :LANES] + product[:, LANES:]
-        w_buf[r0 : r0 + size, :] = placed[0, r0 : r0 + size, :] - factor * placed[1, r0 : r0 + size, :]
+        w_buf[r0 : r0 + size, :] = placed[WEIGHT, r0 : r0 + size, :] - factor * placed[UPDATE, r0 : r0 + size, :]
         window = pl.ds(r0, size)
         copy = pltpu.make_async_copy(w_buf.at[window], w_out.at[window], sems.at[2 + c])
         copy.start()
@@ -390,7 +397,7 @@
     vmem, hbm = spec(pltpu.VMEM), spec(pltpu.HBM)
     bounds = pltpu.SMEM(old_bounds.shape, jnp.int32)
     starts = pltpu.VMEM((1, segs), jnp.int32)
-    rim = pltpu.VMEM((4, BLOCK, LANES), f32)
+    rim = pltpu.VMEM((3, BLOCK, LANES), f32)
     dma = pltpu.SemaphoreType.DMA
     placed, sums, chosen, wide = pl.pallas_call(
         functools.partial(step_kernel, axis, n),
@@ -399,10 +406,10 @@
             jax.ShapeDtypeStruct((4, rows, LANES), f32),
             jax.ShapeDtypeStruct((5, LANES), f32),
             jax.ShapeDtypeStruct((rows, 2 * LANES), jnp.bfloat16),
-            jax.ShapeDtypeStruct((1,), jnp.int32),
+            jax.ShapeDtypeStruct((1, LANES), jnp.int32),
         ),
         in_specs=[hbm] * 7,
-        out_specs=(vmem, vmem, vmem, spec(pltpu.SMEM)),
+        out_specs=(vmem, vmem, vmem, vmem),
         scratch_shapes=[
             pltpu.VMEM((4, rows + 2 * PAD, LANES), f32),
             pltpu.VMEM((rows, LANES), f32),
@@ -410,7 +417,6 @@
             pltpu.VMEM((rows, LANES), grads.dtype),
             pltpu.VMEM((3 * segs, padded), jnp.bfloat16),
             pltpu.VMEM((2, LANES), f32),
-            rim,
             rim,
             rim,
             rim,
@@ -458,7 +464,7 @@
         )(sums)
         return finish(placed, sums, chosen)
 
-    outs = lax.switch(wide.reshape(()), (finish, gather), placed, sums, chosen)
+    outs = lax.switch(wide[0, 0], (finish, gather), placed, sums, chosen)
     return tuple(x.reshape(cap) for x in outs)
 
 

time: 10.4 us -> 9.05 us (0.87)
  the two profiles are of different devices: /device:TPU:1 before, /device:TPU:0 now
where the time goes in v4:
time: 9.05 us; the launch traced here: 8.89 us
  Pallas kernels  8.2 us (91%)
  between operations  0.68 us (8%)
    pallas_call x1, Pallas kernels, shards(): pl.pallas_call(functools.partial(step_kernel, axis, n), name='step', out_...  7.03 us
    pallas_call x1, Pallas kernels, finish(): pl.pallas_call(functools.partial(apply_kernel, segs), name='apply', out_s...  1.16 us

profile of v4, /device:TPU:0, one launch (start us, length us, event | category | flops | bytes accessed | tf_op | source)
XLA Modules:
  0.0 8.9 jit_solution(9848169913306006023)
XLA Ops:
  0.6 7.0 %step.1 = (f32[4,992,128]{2,1,0:T(8,128)S(1)}, f32[5,128]{1,0:T(8,128)S(1)}, bf16[992,256]{1,0:T(8,128)(2,1)S(1)}, s32[1,128]{1,0:T(1,128)S(1)}) custom-call(s32[33]{0:T(128)} %old_hbm.1, s32[33]{0:T(128)} %new_hbm.1, s32[1,64]{1,0:T(1,128)} %bitcast.15, f32[992,128]{1,0:T(8,128)} %bitcast.11, f32[992,128]{1,0:T(8,128)} %bitcast.12, f32[992,128]{1,0:T(8,128)} %bitcast.13, ...), custom_call_target="tpu_custom_call" | custom-call | tf_op jit(solution)/shard_map/step/pallas_call | solution.py:402
  7.7 1.2 %conditional.1 = ((f32[992,128]{1,0:T(8,128)}, f32[992,128]{1,0:T(8,128)}, f32[992,128]{1,0:T(8,128)})) conditional(s32[]{:T(128)} %bitcast.5, (f32[4,992,128]{2,1,0:T(8,128)S(1)}, f32[5,128]{1,0:T(8,128)S(1)}, bf16[992,256]{1,0:T(8,128)(2,1)S(1)}) %tuple.21, (f32[5,128]{1,0:T(8,128)S(1)}, f32[4,992,128]{2,1,0:T(8,128)S(1)}, ...), branch_computations={%region_0.0_spmd.clone, %region_1.0_spmd.clone} | conditional | bytes 8 | solution.py:467
  7.7 1.2 %apply.2 = (f32[992,128]{1,0:T(8,128)}, f32[992,128]{1,0:T(8,128)}, f32[992,128]{1,0:T(8,128)}) custom-call(f32[4,992,128]{2,1,0:T(8,128)S(1)} %get-tuple-element.49.placed, f32[5,128]{1,0:T(8,128)S(1)} %get-tuple-element.50.sums, bf16[992,256]{1,0:T(8,128)(2,1)S(1)} %get-tuple-element.51.chosen), custom_call_target="tpu_custom_call" | custom-call | tf_op jit(solution)/shard_map/cond/branch_0_fun/apply/pallas_call | solution.py:443

commit v5 on v4

--- a/solution.py
+++ b/solution.py
@@ -41,13 +41,13 @@
 
 
 def moved(first, second, lanes):
-    picked = jnp.where(lane_ids() >= lanes, first, second)
+    picked = jnp.where(lane_ids(first.shape[0]) >= lanes, first, second)
     return pltpu.roll(picked, (LANES - lanes) & (LANES - 1), 1)
 
 
-def adaptive(moment, second):
+def inverse(second):
     spread = second * (CORR_ONE * CORR_ONE / CORR_TWO)
-    return moment / (spread * lax.rsqrt(spread) + CORR_ONE * EPSILON)
+    return 1.0 / (spread * lax.rsqrt(spread) + CORR_ONE * EPSILON)
 
 
 def fetched(tables, refs, sems):
@@ -60,7 +60,7 @@
 def step_kernel(
     axis, n, old_hbm, new_hbm, seg_hbm, w_hbm, m_hbm, v_hbm, g_hbm, placed, sums, chosen, wide,
     state, m_buf, v_buf, g_buf, member, part, tail, left_rim, right_rim,
-    before, after, slots, old_ref, new_ref, seg_ref, seg_list, sems, table_sems, send, receive, rim_send, rim_receive,
+    before, after, slots, old_ref, new_ref, seg_ref, sems, table_sems, send, receive, rim_send, rim_receive,
 ):
     rows = m_buf.shape[0]
     blocks = rows // BLOCK
@@ -68,9 +68,9 @@
     me = lax.axis_index(axis)
     right = lax.rem(me + 1, n)
     left = lax.rem(me + n - 1, n)
-    tables = fetched((old_hbm, new_hbm, seg_hbm, seg_hbm), (old_ref, new_ref, seg_ref, seg_list), table_sems)
+    tables = fetched((old_hbm, new_hbm, seg_hbm), (old_ref, new_ref, seg_ref), table_sems)
     weights = state.at[WEIGHT, pl.ds(PAD, rows)]
-    loads = fetched((g_hbm, m_hbm, v_hbm, w_hbm), (g_buf, m_buf, v_buf, weights), sems)
+    loads = fetched((v_hbm, g_hbm, m_hbm, w_hbm), (v_buf, g_buf, m_buf, weights), sems)
     barrier = pltpu.get_barrier_semaphore()
     near = [k for k in range(-REACH, REACH + 1) if k and abs(k) < n]
 
@@ -115,31 +115,29 @@
 
     flat = flat_ids()
 
-    for copy in loads[:3]:
+    spans = [(slice(r0, r0 + BLOCK), slice(r0 + PAD, r0 + PAD + BLOCK)) for r0 in range(0, rows, BLOCK)]
+    for copy in loads[:2]:
         copy.wait()
-    for r0 in range(0, rows, BLOCK):
-        here = slice(r0, r0 + BLOCK)
-        there = slice(r0 + PAD, r0 + PAD + BLOCK)
+    for here, there in spans:
         gradient = g_buf[here, :].astype(jnp.float32)
-        moment = BETA_ONE * m_buf[here, :] + (1.0 - BETA_ONE) * gradient
         second = BETA_TWO * v_buf[here, :] + ((1.0 - BETA_TWO) * gradient) * gradient
-        state[UPDATE, there, :] = adaptive(moment, second)
+        state[UPDATE, there, :] = inverse(second)
+        state[SECOND, there, :] = second
+    loads[2].wait()
+    for here, there in spans:
+        moment = BETA_ONE * m_buf[here, :] + (1.0 - BETA_ONE) * g_buf[here, :].astype(jnp.float32)
+        state[UPDATE, there, :] = moment * state[UPDATE, there, :]
         state[MOMENT, there, :] = moment
-        state[SECOND, there, :] = second
     loads[3].wait()
-    pl.semaphore_wait(barrier, jnp.minimum(me, REACH) + jnp.minimum(n - 1 - me, REACH))
-    start = count - MARGIN
-    start_row = start >> LANE_BITS
-    start_lane = start & (LANES - 1)
+    peers = jnp.minimum(me, REACH) + jnp.minimum(n - 1 - me, REACH)
+    pl.semaphore_wait(barrier, peers)
+    start_row = (count - MARGIN) >> LANE_BITS
     for a in range(3):
-        tail[a] = moved(
-            state[a + 1, pl.ds(PAD + start_row, BLOCK), :],
-            state[a + 1, pl.ds(PAD + start_row + 1, BLOCK), :],
-            start_lane,
-        )
+        tail[a] = state[a + 1, pl.ds(PAD + start_row, BLOCK + 8), :]
+    ragged = pl.ds(0, BLOCK + 1)
     onward = pltpu.make_async_remote_copy(
-        src_ref=tail,
-        dst_ref=left_rim,
+        src_ref=tail.at[:, ragged],
+        dst_ref=left_rim.at[:, ragged],
         send_sem=rim_send.at[0],
         recv_sem=rim_receive.at[0],
         device_id=(right,),
@@ -199,8 +197,8 @@
         return pltpu.make_async_remote_copy(
             src_ref=part,
             dst_ref=slots.at[k + REACH],
-            send_sem=send.at[k + REACH],
-            recv_sem=receive.at[k + REACH],
+            send_sem=send,
+            recv_sem=receive,
             device_id=(me + k,),
             device_id_type=MESH,
         )
@@ -254,11 +252,9 @@
     lax.fori_loop(0, blocks, choose, 0, unroll=2)
     sums[2:3, :] = jnp.full((1, LANES), new_phase, jnp.int32).astype(jnp.float32)
 
-    def longest(s, most):
-        return jnp.maximum(most, seg_list[0, s + 1] - seg_list[0, s])
-
-    most = lax.fori_loop(0, segs - 1, longest, old_ref[n] - seg_list[0, segs - 1], unroll=9)
-    wide[...] = jnp.full((1, LANES), jnp.where(most > REACH * (rows * LANES - 2 * MARGIN) - MARGIN, 1, 0), jnp.int32)
+    length = jnp.where(line == segs - 1, old_ref[n] >> HALF_BITS, past) - first
+    most = (REACH * (rows * LANES - 2 * MARGIN) - MARGIN) >> HALF_BITS
+    wide[...] = jnp.max(jnp.where(length > most, 1, 0), axis=0, keepdims=True)
 
     @pl.when(me < n - 1)
     def end_right():
@@ -270,10 +266,19 @@
         back.wait_send()
         onward.wait_recv()
 
-    for ref, there, rim in ((before, slice(0, BLOCK), left_rim), (after, slice(PAD, PAD + BLOCK), right_rim)):
+    left_start = low - old_ref[jnp.maximum(me - 1, 0)] - MARGIN
+    left_lane = left_start & (LANES - 1)
+    left_rows = [moved(left_rim[a, 0:BLOCK, :], left_rim[a, 1 : BLOCK + 1, :], left_lane) for a in range(3)]
+    right_rows = [right_rim[a] for a in range(3)]
+    for ref, there, rim in ((before, slice(0, BLOCK), left_rows), (after, slice(PAD, PAD + BLOCK), right_rows)):
         for a in range(3):
             ref[a + 1, there, :] = rim[a]
-        ref[UPDATE, there, :] = adaptive(rim[1], rim[2]) + DECAY * rim[0]
+        ref[UPDATE, there, :] = rim[1] * inverse(rim[2]) + DECAY * rim[0]
+    side = (shift - count) & (LANES - 1)
+    for a in range(4):
+        after[a, PAD - 8 : PAD + BLOCK, :] = moved(
+            after[a, PAD - 8 : PAD + BLOCK, :], after[a, PAD - 7 : PAD + BLOCK + 1, :], side
+        )
     for a in range(4):
         placed[a, 0:BLOCK, :] = moved(
             before[a, pl.ds(BLOCK + top, BLOCK), :], before[a, pl.ds(BLOCK + top + 1, BLOCK), :], lanes
@@ -282,28 +287,26 @@
     for b in range(blocks - 3, blocks):
         offset = b * MARGIN + shift - count
         edge = jnp.clip(offset >> LANE_BITS, -PAD, PAD - 7) + PAD
-        side = offset & (LANES - 1)
         index = flat + b * MARGIN
         beyond = (index + shift >= count) & (index < new_count)
         here = slice(b * BLOCK, (b + 1) * BLOCK)
         for a in range(4):
-            rim = moved(after[a, pl.ds(edge, BLOCK), :], after[a, pl.ds(edge + 1, BLOCK), :], side)
-            placed[a, here, :] = jnp.where(beyond, rim, placed[a, here, :])
-
+            placed[a, here, :] = jnp.where(beyond, after[a, pl.ds(edge, BLOCK), :], placed[a, here, :])
+
+    def settle(semaphore):
+        for c in sorted({min(i, REACH) + min(n - 1 - i, REACH) for i in range(n)}):
+
+            @pl.when(peers == c)
+            def end(c=c):
+                some = slots.at[pl.ds(0, c)]
+                pltpu.make_async_copy(some, some, semaphore).wait()
+
+    settle(send)
+    settle(receive)
     total = part[...]
     for k in near:
-
-        @pl.when(inside(-k))
-        def get_sums(k=k):
-            tell(k).wait_recv()
-
         total = total + jnp.where(inside(-k), slots[k + REACH], 0.0)
     sums[0:2, :] = total
-    for k in near:
-
-        @pl.when(inside(k))
-        def end_sums(k=k):
-            tell(k).wait_send()
 
 
 def everyone_kernel(axis, n, near_sums, sums, part, slots, send, receive):
@@ -398,6 +401,7 @@
     bounds = pltpu.SMEM(old_bounds.shape, jnp.int32)
     starts = pltpu.VMEM((1, segs), jnp.int32)
     rim = pltpu.VMEM((3, BLOCK, LANES), f32)
+    ragged = pltpu.VMEM((3, BLOCK + 8, LANES), f32)
     dma = pltpu.SemaphoreType.DMA
     placed, sums, chosen, wide = pl.pallas_call(
         functools.partial(step_kernel, axis, n),
@@ -417,8 +421,8 @@
             pltpu.VMEM((rows, LANES), grads.dtype),
             pltpu.VMEM((3 * segs, padded), jnp.bfloat16),
             pltpu.VMEM((2, LANES), f32),
-            rim,
-            rim,
+            ragged,
+            ragged,
             rim,
             pltpu.VMEM((4, EDGE, LANES), f32),
             pltpu.VMEM((4, EDGE, LANES), f32),
@@ -426,11 +430,10 @@
             bounds,
             bounds,
             starts,
-            pltpu.SMEM((1, segs), jnp.int32),
             dma((4,)),
-            dma((4,)),
-            dma((2 * REACH + 1,)),
-            dma((2 * REACH + 1,)),
+            dma((3,)),
+            dma,
+            dma,
             dma((2,)),
             dma((2,)),
         ],

time: 9.05 us -> 8.81 us (0.973)
  Pallas kernels: 8.2 us -> 7.96 us
    pallas_call x1, Pallas kernels: 7.03 us -> 6.8 us  [shards(): pl.pallas_call(functools.partial(step_kernel, axis, n), name='step', out_...]
where the time goes in v5:
time: 8.81 us; the launch traced here: 8.66 us
  Pallas kernels  7.96 us (90%)
  between operations  0.68 us (8%)
    pallas_call x1, Pallas kernels, shards(): pl.pallas_call(functools.partial(step_kernel, axis, n), name='step', out_...  6.8 us
    pallas_call x1, Pallas kernels, finish(): pl.pallas_call(functools.partial(apply_kernel, segs), name='apply', out_s...  1.16 us

profile of v5, /device:TPU:0, one launch (start us, length us, event | category | flops | bytes accessed | tf_op | source)
XLA Modules:
  0.0 8.7 jit_solution(666763040123228162)
XLA Ops:
  0.6 6.8 %step.1 = (f32[4,992,128]{2,1,0:T(8,128)S(1)}, f32[5,128]{1,0:T(8,128)S(1)}, bf16[992,256]{1,0:T(8,128)(2,1)S(1)}, s32[1,128]{1,0:T(1,128)S(1)}) custom-call(s32[33]{0:T(128)} %old_hbm.1, s32[33]{0:T(128)} %new_hbm.1, s32[1,64]{1,0:T(1,128)} %bitcast.15, f32[992,128]{1,0:T(8,128)} %bitcast.11, f32[992,128]{1,0:T(8,128)} %bitcast.12, f32[992,128]{1,0:T(8,128)} %bitcast.13, ...), custom_call_target="tpu_custom_call" | custom-call | tf_op jit(solution)/shard_map/step/pallas_call | solution.py:406
  7.5 1.2 %conditional.1 = ((f32[992,128]{1,0:T(8,128)}, f32[992,128]{1,0:T(8,128)}, f32[992,128]{1,0:T(8,128)})) conditional(s32[]{:T(128)} %bitcast.5, (f32[4,992,128]{2,1,0:T(8,128)S(1)}, f32[5,128]{1,0:T(8,128)S(1)}, bf16[992,256]{1,0:T(8,128)(2,1)S(1)}) %tuple.21, (f32[5,128]{1,0:T(8,128)S(1)}, f32[4,992,128]{2,1,0:T(8,128)S(1)}, ...), branch_computations={%region_0.0_spmd.clone, %region_1.0_spmd.clone} | conditional | bytes 8 | solution.py:470
  7.5 1.2 %apply.2 = (f32[992,128]{1,0:T(8,128)}, f32[992,128]{1,0:T(8,128)}, f32[992,128]{1,0:T(8,128)}) custom-call(f32[4,992,128]{2,1,0:T(8,128)S(1)} %get-tuple-element.49.placed, f32[5,128]{1,0:T(8,128)S(1)} %get-tuple-element.50.sums, bf16[992,256]{1,0:T(8,128)(2,1)S(1)} %get-tuple-element.51.chosen), custom_call_target="tpu_custom_call" | custom-call | tf_op jit(solution)/shard_map/cond/branch_0_fun/apply/pallas_call | solution.py:446

commit v6 on v5

--- a/solution.py
+++ b/solution.py
@@ -15,7 +15,7 @@
 LANE_BITS = 7
 PAD = BLOCK + 8
 EDGE = 2 * PAD + BLOCK
-TILE = 256
+TILE = 1024
 REACH = 4
 UPDATE, WEIGHT, MOMENT, SECOND = range(4)
 
@@ -60,7 +60,7 @@
 def step_kernel(
     axis, n, old_hbm, new_hbm, seg_hbm, w_hbm, m_hbm, v_hbm, g_hbm, placed, sums, chosen, wide,
     state, m_buf, v_buf, g_buf, member, part, tail, left_rim, right_rim,
-    before, after, slots, old_ref, new_ref, seg_ref, sems, table_sems, send, receive, rim_send, rim_receive,
+    before, after, slots, old_ref, new_ref, seg_ref, sems, send, receive, rim_send, rim_receive,
 ):
     rows = m_buf.shape[0]
     blocks = rows // BLOCK
@@ -68,7 +68,13 @@
     me = lax.axis_index(axis)
     right = lax.rem(me + 1, n)
     left = lax.rem(me + n - 1, n)
-    tables = fetched((old_hbm, new_hbm, seg_hbm), (old_ref, new_ref, seg_ref), table_sems)
+    tables = [
+        pltpu.make_async_copy(old_hbm, old_ref, rim_send.at[0]),
+        pltpu.make_async_copy(new_hbm, new_ref, rim_send.at[1]),
+        pltpu.make_async_copy(seg_hbm, seg_ref, send),
+    ]
+    for copy in tables:
+        copy.start()
     weights = state.at[WEIGHT, pl.ds(PAD, rows)]
     loads = fetched((v_hbm, g_hbm, m_hbm, w_hbm), (v_buf, g_buf, m_buf, weights), sems)
     barrier = pltpu.get_barrier_semaphore()
@@ -431,7 +437,6 @@
             bounds,
             starts,
             dma((4,)),
-            dma((3,)),
             dma,
             dma,
             dma((2,)),

time: 8.81 us -> 8.77 us (level)
  no operation moved by 1% of the time
where the time goes in v6:
time: 8.77 us; the launch traced here: 8.62 us
  Pallas kernels  7.92 us (90%)
  between operations  0.68 us (8%)
    pallas_call x1, Pallas kernels, shards(): pl.pallas_call(functools.partial(step_kernel, axis, n), name='step', out_...  6.76 us
    pallas_call x1, Pallas kernels, finish(): pl.pallas_call(functools.partial(apply_kernel, segs), name='apply', out_s...  1.16 us

profile of v6, /device:TPU:0, one launch (start us, length us, event | category | flops | bytes accessed | tf_op | source)
XLA Modules:
  0.0 8.6 jit_solution(15592146479575374375)
XLA Ops:
  0.6 6.8 %step.1 = (f32[4,992,128]{2,1,0:T(8,128)S(1)}, f32[5,128]{1,0:T(8,128)S(1)}, bf16[992,256]{1,0:T(8,128)(2,1)S(1)}, s32[1,128]{1,0:T(1,128)S(1)}) custom-call(s32[33]{0:T(128)} %old_hbm.1, s32[33]{0:T(128)} %new_hbm.1, s32[1,64]{1,0:T(1,128)} %bitcast.15, f32[992,128]{1,0:T(8,128)} %bitcast.11, f32[992,128]{1,0:T(8,128)} %bitcast.12, f32[992,128]{1,0:T(8,128)} %bitcast.13, ...), custom_call_target="tpu_custom_call" | custom-call | tf_op jit(solution)/shard_map/step/pallas_call | solution.py:412
  7.4 1.2 %conditional.1 = ((f32[992,128]{1,0:T(8,128)}, f32[992,128]{1,0:T(8,128)}, f32[992,128]{1,0:T(8,128)})) conditional(s32[]{:T(128)} %bitcast.5, (f32[4,992,128]{2,1,0:T(8,128)S(1)}, f32[5,128]{1,0:T(8,128)S(1)}, bf16[992,256]{1,0:T(8,128)(2,1)S(1)}) %tuple.21, (f32[5,128]{1,0:T(8,128)S(1)}, f32[4,992,128]{2,1,0:T(8,128)S(1)}, ...), branch_computations={%region_0.0_spmd.clone, %region_1.0_spmd.clone} | conditional | bytes 8 | solution.py:475
  7.4 1.2 %apply.2 = (f32[992,128]{1,0:T(8,128)}, f32[992,128]{1,0:T(8,128)}, f32[992,128]{1,0:T(8,128)}) custom-call(f32[4,992,128]{2,1,0:T(8,128)S(1)} %get-tuple-element.49.placed, f32[5,128]{1,0:T(8,128)S(1)} %get-tuple-element.50.sums, bf16[992,256]{1,0:T(8,128)(2,1)S(1)} %get-tuple-element.51.chosen), custom_call_target="tpu_custom_call" | custom-call | tf_op jit(solution)/shard_map/cond/branch_0_fun/apply/pallas_call | solution.py:451
